TPU v7x, 256 devices: a whole 4x4x8 slice. The times are simulated.
256 devices in a mesh: dp: 8 (over x, core), expert: 32 (over z, y).
Axes of the slice: x: 4, y: 4, z: 8, core: 2. Of those that a mesh axis runs over, the one named last changes fastest.
Arguments:
- tokens: bfloat16 [2048, 6144], P('dp', 'expert'), may hold values from -6 to 6
- cotangent: bfloat16 [2048, 6144], P('dp', 'expert'), may hold values from -6 to 6
- expert_choice: int32 [2048, 2], P('dp'), may hold values from 0 to 7, all different within a row; in each aligned block of 256 rows (0 to 255, 256 to 511, ...) at most 80 rows name the same one
- gate_values: bfloat16 [2048, 2], P('dp'), may hold values from 0.099609375 to 1
- gate_weight: bfloat16 [8, 6144, 8192], P('dp', None, 'expert'), may hold values from -0.078125 to 0.078125
- up_weight: bfloat16 [8, 6144, 8192], P('dp', None, 'expert'), may hold values from -0.078125 to 0.078125
- down_weight: bfloat16 [8, 8192, 6144], P('dp', 'expert'), may hold values from -0.0625 to 0.0625
- shrinker: bfloat16 [8, 32, 6144], P('dp'), may hold values from -0.078125 to 0.078125
- widener: bfloat16 [8, 2, 16, 8192], P('dp', None, None, 'expert'), may hold values from -0.375 to 0.375
- squeezer: bfloat16 [8, 16, 8192], P('dp', None, 'expert'), may hold values from -0.0625 to 0.0625
- spreader: bfloat16 [8, 16, 6144], P('dp'), may hold values from -0.375 to 0.375
Outputs:
- token_grad: bfloat16 [2048, 6144], P('dp', 'expert')
- gate_grad: float32 [2048, 2], P('dp')
- shrinker_grad: float32 [8, 32, 6144], P('dp')
- widener_grad: float32 [8, 2, 16, 8192], P('dp', None, None, 'expert')
- squeezer_grad: float32 [8, 16, 8192], P('dp', None, 'expert')
- spreader_grad: float32 [8, 16, 6144], P('dp')
Inputs may be any that keep to these rules, and one draw needn't show every extreme that they name: `expert_choice`: each row names 2 different experts. Among the 256 tokens of one index of dp no expert is chosen more than 80 times, and some expert is chosen exactly 80 times by the tokens of some or all indices of dp.
All inputs are finite; a program needn't handle non-finite values.
Results may differ from a plain program's by a relative error of at most 0.02.
Values may be sent and summed in bfloat16 or wider, within the bound.
No kernel may reach another device: no remote copies, remote signals or barrier semaphores. Data moves between devices by JAX's collectives and lax.ppermute only.
A program may use at most 128 MiB of HBM per device.

v0:
```python
import jax
import jax.numpy as jnp
from jax import lax
from jax.sharding import PartitionSpec as P

adapter_scale = 2.0


def product(pattern, operand_a, operand_b):
    return jnp.einsum(pattern, operand_a, operand_b, preferred_element_type=jnp.float32)


def silu_pair(gate_pre):
    logistic = jax.nn.sigmoid(gate_pre)
    return (gate_pre * logistic, logistic * (1.0 + gate_pre * (1.0 - logistic)))


def full_rows(gathered, capacity, part_width):
    n_groups = gathered.shape[0]
    n_sources = gathered.shape[1]
    ordered = gathered.reshape(n_groups, n_sources, capacity, part_width).transpose(1, 2, 0, 3)
    return ordered.reshape(n_sources * capacity, n_groups * part_width)


def local(
    tokens,
    cotangent,
    expert_choice,
    gate_values,
    gate_weight,
    up_weight,
    down_weight,
    shrinker,
    widener,
    squeezer,
    spreader,
):
    tok_rows, part_width = tokens.shape
    top_k = expert_choice.shape[1]
    low_rank = spreader.shape[1]
    n_groups = lax.axis_size("expert")
    n_experts = lax.axis_size("dp")
    capacity = tok_rows * top_k * 5 // (4 * n_experts)
    own_rows = n_experts * capacity
    flat_choice = expert_choice.reshape(-1)
    onehot = (flat_choice[:, None] == jnp.arange(n_experts, dtype=jnp.int32)[None, :]).astype(
        jnp.int32
    )
    before = jnp.cumsum(onehot, axis=0) - onehot
    slot_index = jnp.sum(before * onehot, axis=1)
    target = flat_choice * capacity + slot_index
    placing = target[None, :] == jnp.arange(own_rows, dtype=jnp.int32)[:, None]
    stacked = jnp.repeat(jnp.concatenate([tokens, cotangent], axis=1), top_k, axis=0)
    placed = jnp.dot(
        placing.astype(jnp.bfloat16), stacked, preferred_element_type=jnp.float32
    ).astype(jnp.bfloat16)
    send_x = placed[:, :part_width].reshape(n_experts, capacity * part_width)
    send_dy = placed[:, part_width:].reshape(n_experts, capacity * part_width)
    gate_flat = gate_values.reshape(-1).astype(jnp.float32)
    send_gate = (
        jnp.sum(jnp.where(placing, gate_flat[None, :], 0.0), axis=1)
        .astype(jnp.bfloat16)
        .reshape(n_experts, capacity)
    )
    recv_x, recv_dy, recv_gate = (
        lax.all_to_all(send_x, "dp", split_axis=0, concat_axis=0, tiled=True),
        lax.all_to_all(send_dy, "dp", split_axis=0, concat_axis=0, tiled=True),
        lax.all_to_all(send_gate, "dp", split_axis=0, concat_axis=0, tiled=True),
    )
    gate_rows = recv_gate.reshape(-1).astype(jnp.float32)
    gathered_x, gathered_dy = (
        lax.all_gather(recv_x[None], "expert", axis=0, tiled=True),
        lax.all_gather(recv_dy[None], "expert", axis=0, tiled=True),
    )
    rows_dy = full_rows(gathered_dy, capacity, part_width)
    rows_x = full_rows(gathered_x, capacity, part_width)
    shrink_local = shrinker[0]
    widen_local = widener[0]
    squeeze_local = squeezer[0]
    spread_local = spreader[0]
    lowrank_in = product("nd,rd->nr", rows_x, shrink_local).astype(jnp.bfloat16)
    gate_pre = jnp.dot(
        rows_x, gate_weight[0], preferred_element_type=jnp.float32
    ) + adapter_scale * jnp.dot(
        lowrank_in[:, :low_rank], widen_local[0], preferred_element_type=jnp.float32
    )
    up_pre = jnp.dot(
        rows_x, up_weight[0], preferred_element_type=jnp.float32
    ) + adapter_scale * jnp.dot(
        lowrank_in[:, low_rank:], widen_local[1], preferred_element_type=jnp.float32
    )
    silu_gate, silu_slope = silu_pair(gate_pre)
    activation = (silu_gate * up_pre).astype(jnp.bfloat16)
    out_part = product("rf,nf->rn", squeeze_local, activation)
    out_low = lax.psum(out_part.astype(jnp.bfloat16), "expert").astype(jnp.float32)
    back_down = product("nd,fd->nf", rows_dy, down_weight[0])
    back_low = product("rd,nd->rn", spread_local, rows_dy)
    gate_part = jnp.sum(activation.astype(jnp.float32) * back_down, axis=1)
    scaled_low = (back_low * gate_rows[None, :]).astype(jnp.bfloat16)
    act_delta = gate_rows[:, None] * back_down + adapter_scale * product(
        "rn,rf->nf", scaled_low, squeeze_local
    )
    gate_delta = (act_delta * up_pre * silu_slope).astype(jnp.bfloat16)
    up_delta = (act_delta * silu_gate).astype(jnp.bfloat16)
    back_part = jnp.concatenate(
        [
            product("rf,nf->rn", widen_local[0], gate_delta),
            product("rf,nf->rn", widen_local[1], up_delta),
        ],
        axis=0,
    )
    back_sum, gate_sum = (
        lax.psum(back_part.astype(jnp.bfloat16), "expert").astype(jnp.float32),
        lax.psum(gate_part.astype(jnp.bfloat16), "expert").astype(jnp.float32),
    )
    low_out = out_low.astype(jnp.bfloat16)
    gate_dots = gate_sum + adapter_scale * jnp.sum(low_out.astype(jnp.float32) * back_low, axis=0)
    back_in = back_sum.astype(jnp.bfloat16)
    gate_blocks = gate_weight[0].reshape(n_groups, part_width, gate_weight.shape[2])
    up_blocks = up_weight[0].reshape(n_groups, part_width, up_weight.shape[2])
    term = product("nf,kdf->knd", gate_delta, gate_blocks) + product(
        "nf,kdf->knd", up_delta, up_blocks
    )
    token_part = (
        lax.psum_scatter(
            term.reshape(1 * lax.axis_size("expert"), own_rows * part_width).astype(jnp.bfloat16),
            "expert",
            scatter_dimension=0,
            tiled=True,
        )
        .astype(jnp.float32)
        .reshape(own_rows, part_width)
    )
    shrink_cols = lax.dynamic_slice_in_dim(
        shrink_local, lax.axis_index("expert") * part_width, part_width, 1
    )
    token_part = token_part + adapter_scale * product("rn,rd->nd", back_in, shrink_cols)
    token_back, gate_back = (
        lax.all_to_all(
            token_part.reshape(n_experts, capacity * part_width).astype(jnp.bfloat16),
            "dp",
            split_axis=0,
            concat_axis=0,
            tiled=True,
        ).astype(jnp.float32),
        lax.all_to_all(
            gate_dots.reshape(n_experts, capacity).astype(jnp.bfloat16),
            "dp",
            split_axis=0,
            concat_axis=0,
            tiled=True,
        ).astype(jnp.float32),
    )
    picked = jnp.take(token_back.reshape(own_rows, part_width), target, axis=0)
    token_grad = jnp.sum(picked.reshape(tok_rows, top_k, part_width), axis=1).astype(jnp.bfloat16)
    gate_grad = jnp.take(gate_back.reshape(own_rows), target).reshape(tok_rows, top_k)
    shrinker_grad = adapter_scale * product("rn,nd->rd", back_in, rows_x)
    widener_grad = adapter_scale * jnp.stack(
        [
            product("nr,nf->rf", lowrank_in[:, :low_rank], gate_delta),
            product("nr,nf->rf", lowrank_in[:, low_rank:], up_delta),
        ]
    )
    squeezer_grad = adapter_scale * product("rn,nf->rf", scaled_low, activation)
    weighted_low = (out_low * gate_rows[None, :]).astype(jnp.bfloat16)
    spreader_grad = adapter_scale * product("rn,nd->rd", weighted_low, rows_dy)
    return (
        token_grad,
        gate_grad,
        shrinker_grad[None],
        widener_grad[None],
        squeezer_grad[None],
        spreader_grad[None],
    )


def solution(mesh):
    placed = (
        P("dp", "expert"),
        P("dp", "expert"),
        P("dp", None),
        P("dp", None),
        P("dp", None, "expert"),
        P("dp", None, "expert"),
        P("dp", "expert", None),
        P("dp", None, None),
        P("dp", None, None, "expert"),
        P("dp", None, "expert"),
        P("dp", None, None),
    )
    return jax.shard_map(
        local,
        mesh=mesh,
        in_specs=placed,
        out_specs=(
            P("dp", "expert"),
            P("dp", None),
            P("dp", None, None),
            P("dp", None, None, "expert"),
            P("dp", None, "expert"),
            P("dp", None, None),
        ),
        check_vma=False,
    )
```

profile of v0, /device:TPU:1, one launch (start us, length us, event | category | flops | bytes accessed | tf_op | source)
XLA Modules:
  0.0 594.0 jit_solution(10980135344185267276)
XLA Ops:
  25.2 12.8 %all_to_all.38 = bf16[8,2,7680]{2,1,0:T(2,128)(2,1)S(1)} all-to-all(bf16[8,2,7680]{2,1,0:T(2,128)(2,1)} %reshape.290), channel_id=1, replica_groups=mesh['dp'=8,'expert'=32] {'dp'}, dimensions={0} | all-to-all | bytes 491520 | tf_op jit(solution)/shard_map/all_to_all | solution.py:67
  48.7 10.7 %all_to_all.39 = bf16[8,2,7680]{2,1,0:T(2,128)(2,1)S(1)} all-to-all(bf16[8,2,7680]{2,1,0:T(2,128)(2,1)} %reshape.288), channel_id=1, replica_groups=mesh['dp'=8,'expert'=32] {'dp'}, dimensions={0} | all-to-all | bytes 491520 | tf_op jit(solution)/shard_map/all_to_all | solution.py:66
  62.7 8.1 %all_to_all.40 = bf16[8,1,80]{2,1,0:T(2,128)(2,1)S(1)} all-to-all(bf16[8,1,80]{2,1,0:T(2,128)(2,1)S(1)} %convert_element_type.180), channel_id=1, replica_groups=mesh['dp'=8,'expert'=32] {'dp'}, dimensions={0} | all-to-all | bytes 2560 | tf_op jit(solution)/shard_map/all_to_all | solution.py:68
  70.9 65.3 %all-gather.5.cloned.1.call-done = bf16[256,1,15360]{2,0,1:T(8,128)(2,1)} async-done(((bf16[8,1,15360]{2,0,1:T(8,128)(2,1)}), bf16[256,1,15360]{2,0,1:T(8,128)(2,1)}) %all-gather.5.cloned.1.call-update) | async-done | bytes 7864336 | tf_op jit(solution)/shard_map/all_gather | solution.py:73
  136.2 18.1 %reshape.231 = bf16[32,8,80,192]{3,2,1,0:T(8,128)(2,1)} reshape(bf16[256,1,15360]{2,0,1:T(8,128)(2,1)} %all-gather.5.cloned.1.call-done) | data formatting | bytes 15728640 | tf_op jit(solution)/shard_map/reshape | solution.py:21
  154.3 13.9 %copy.93 = bf16[8,80,32,192]{3,2,1,0:T(8,128)(2,1)} copy(bf16[8,80,32,192]{3,1,0,2:T(8,128)(2,1)} %bitcast.103) | data formatting | bytes 15728640 | tf_op jit(solution)/shard_map/transpose | solution.py:21
  168.2 18.2 %reshape.232 = bf16[640,6144]{1,0:T(8,128)(2,1)} reshape(bf16[8,80,32,192]{3,2,1,0:T(8,128)(2,1)} %copy.93) | data formatting | bytes 15728640 | tf_op jit(solution)/shard_map/reshape | solution.py:22
  186.4 6.0 %convolution_bitcast_fusion = f32[16,640]{1,0:T(8,128)S(1)} fusion(bf16[640,6144]{1,0:T(8,128)(2,1)} %reshape.232, bf16[1,16,6144]{2,1,0:T(8,128)(2,1)S(1)} %copy-done.8), kind=kOutput, calls=%fused_computation.28 | convolution fusion | flops 125829120 | bytes 8101888 | tf_op jit(solution)/shard_map/rd,nd->rn/dot_general | solution.py:10
  192.4 5.4 fusion.7
  197.8 33.9 %all-gather.7.cloned.1.call-done = bf16[256,1,15360]{2,0,1:T(8,128)(2,1)} async-done(((bf16[8,1,15360]{2,0,1:T(8,128)(2,1)}), bf16[256,1,15360]{2,0,1:T(8,128)(2,1)}) %all-gather.7.cloned.1.call-update) | async-done | bytes 7864336 | tf_op jit(solution)/shard_map/all_gather | solution.py:72
  231.7 18.3 %reshape.233 = bf16[32,8,80,192]{3,2,1,0:T(8,128)(2,1)} reshape(bf16[256,1,15360]{2,0,1:T(8,128)(2,1)} %all-gather.7.cloned.1.call-done) | data formatting | bytes 15728640 | tf_op jit(solution)/shard_map/reshape | solution.py:21
  249.9 13.8 %copy.98 = bf16[8,80,32,192]{3,2,1,0:T(8,128)(2,1)} copy(bf16[8,80,32,192]{3,1,0,2:T(8,128)(2,1)} %bitcast.104) | data formatting | bytes 15728640 | tf_op jit(solution)/shard_map/transpose | solution.py:21
  263.8 18.5 %reshape.234 = bf16[640,6144]{1,0:T(8,128)(2,1)} reshape(bf16[8,80,32,192]{3,2,1,0:T(8,128)(2,1)} %copy.98) | data formatting | bytes 15728640 | tf_op jit(solution)/shard_map/reshape | solution.py:22
  282.3 5.8 convolution_convert_fusion
  295.9 6.8 %fusion.25 = f32[640,32,192]{0,2,1:T(8,128)} fusion(bf16[32,192,256]{2,1,0:T(8,128)(2,1)S(1)} %bitcast.102, bf16[640,256]{0,1:T(8,128)(2,1)S(1)} %get-tuple-element.37), kind=kOutput, calls=%fused_computation.53 | convolution fusion | flops 2013265920 | bytes 19202048 | tf_op jit(solution)/shard_map/nf,kdf->knd/dot_general | solution.py:10
  302.7 8.8 %fusion.2 = bf16[32,640,192]{1,2,0:T(8,128)(2,1)} fusion(f32[640,32,192]{0,2,1:T(8,128)} %fusion.25, bf16[32,192,256]{2,1,0:T(8,128)(2,1)S(1)} %bitcast.105, bf16[640,256]{0,1:T(8,128)(2,1)S(1)} %get-tuple-element.38), kind=kOutput, calls=%fused_computation.7 | convolution fusion | flops 2021130240 | bytes 27066368 | tf_op jit(solution)/shard_map/nf,kdf->knd/dot_general | solution.py:10
  311.6 13.7 %copy.101 = bf16[32,640,192]{2,1,0:T(8,128)(2,1)} copy(bf16[32,640,192]{1,2,0:T(8,128)(2,1)} %fusion.2) | data formatting | bytes 15728640 | tf_op jit(solution)/shard_map/convert_element_type | solution.py:126
  325.3 15.6 %convert_element_type.158 = bf16[32,122880]{1,0:T(8,128)(2,1)} reshape(bf16[32,640,192]{2,1,0:T(8,128)(2,1)} %copy.101) | data formatting | bytes 15728640 | tf_op jit(solution)/shard_map/convert_element_type | solution.py:126
  345.9 114.8 %all-reduce.1 = (bf16[32,640]{1,0:T(8,128)(2,1)S(1)}, bf16[16,640]{1,0:T(8,128)(2,1)S(1)}, bf16[640]{0:T(1024)(128)(2,1)S(1)}) all-reduce(bf16[32,640]{1,0:T(8,128)(2,1)S(1)} %pad_maximum_fusion.1, bf16[16,640]{1,0:T(8,128)(2,1)S(1)} %fusion.18, bf16[640]{0:T(1024)(128)(2,1)S(1)} %get-tuple-element.35), channel_id=1, replica_groups=mesh['dp'=8,'expert'=32] {'expert'}, use_global_device_ids=true, to_apply=%region_5.6 | all-reduce | flops 31360 | bytes 125440 | tf_op jit(solution)/shard_map/psum | solution.py:113
  461.4 32.7 %all-to-all-start.4 = ((bf16[8,1,80]{2,1,0:T(2,128)(2,1)}), bf16[8,1,80]{2,1,0:T(2,128)(2,1)S(1)}, u32[]{:S(2)}, u32[]{:S(2)}) async-start(bf16[8,1,80]{2,1,0:T(2,128)(2,1)} %convert_element_type.182), calls=%async_computation.4 | async-start | bytes 8192 | tf_op jit(solution)/shard_map/all_to_all | solution.py:146
  498.3 5.3 fusion.1
  503.5 5.7 fusion
  513.0 30.8 %all-reduce.4.cloned.1.call-done = bf16[32,122880]{1,0:T(8,128)(2,1)} async-done(((bf16[32,122880]{1,0:T(8,128)(2,1)}), bf16[32,122880]{1,0:T(8,128)(2,1)}) %all-reduce.4.cloned.1.call-update) | async-done | bytes 7864336
  560.7 5.4 all-to-all-start.3
  (114 shorter events, 91.4 us)
Async XLA Ops:
  7.2 280.9 %copy-start = (bf16[1,6144,256]{2,1,0:T(8,128)(2,1)S(1)}, bf16[1,6144,256]{2,1,0:T(8,128)(2,1)}, u32[]{:S(2)}) copy-start(bf16[1,6144,256]{2,1,0:T(8,128)(2,1)} %param.15) | copy-start | bytes 9437188
  7.2 54.9 %copy-start.12 = (bf16[256,2]{0,1:T(2,128)(2,1)S(1)}, bf16[256,2]{0,1:T(2,128)(2,1)}, u32[]{:S(2)}) copy-start(bf16[256,2]{0,1:T(2,128)(2,1)} %param.14) | copy-start | bytes 3076
  7.2 129.0 %all-gather.5.cloned.1.call-start = ((), (), s32[]{:S(2)}) async-start(), calls=%async_computation.5 | async-start | bytes 8110080 | tf_op jit(solution)/shard_map/all_gather | solution.py:73
  40.8 190.9 %all-gather.7.cloned.1.call-start = ((), (), s32[]{:S(2)}) async-start(), calls=%async_computation.6 | async-start | bytes 8110080 | tf_op jit(solution)/shard_map/all_gather | solution.py:72
  62.1 481.8 %all-reduce.4.cloned.1.call-start = ((), (), s32[]{:S(2)}) async-start(), calls=%async_computation.7 | async-start | bytes 15728640
  168.2 18.2 %copy-start.8 = (bf16[1,16,6144]{2,1,0:T(8,128)(2,1)S(1)}, bf16[1,16,6144]{2,1,0:T(8,128)(2,1)}, u32[]{:S(2)}) copy-start(bf16[1,16,6144]{2,1,0:T(8,128)(2,1)} %param.21) | copy-start | bytes 589828
  186.4 6.0 %copy-start.1 = (bf16[640,6144]{1,0:T(8,128)(2,1)S(1)}, bf16[640,6144]{1,0:T(8,128)(2,1)}, u32[]{:S(2)}) copy-start(bf16[640,6144]{1,0:T(8,128)(2,1)} %reshape.232) | copy-start | bytes 23592964
  282.3 5.8 copy-start.2
  288.1 2.9 copy-start.3
  291.0 3.0 copy-start.10
  291.0 3.3 copy-start.6
  291.0 3.3 copy-start.11
  295.9 6.8 %copy-start.5 = (bf16[640,256]{0,1:T(8,128)(2,1)}, bf16[640,256]{0,1:T(8,128)(2,1)S(1)}, u32[]{:S(2)}) copy-start(bf16[640,256]{0,1:T(8,128)(2,1)S(1)} %get-tuple-element.37) | copy-start | bytes 983044
  295.9 6.8 %copy-start.4 = (bf16[640,256]{0,1:T(8,128)(2,1)}, bf16[640,256]{0,1:T(8,128)(2,1)S(1)}, u32[]{:S(2)}) copy-start(bf16[640,256]{0,1:T(8,128)(2,1)S(1)} %get-tuple-element.38) | copy-start | bytes 983044
  340.8 1.0 copy-start.13
  460.7 48.6 %copy-start.7 = (bf16[32,640]{1,0:T(8,128)(2,1)}, bf16[32,640]{1,0:T(8,128)(2,1)S(1)}, u32[]{:S(2)}) copy-start(bf16[32,640]{1,0:T(8,128)(2,1)S(1)} %get-tuple-element.30) | copy-start | bytes 122884
  461.4 48.5 %all-to-all-start.4 = ((bf16[8,1,80]{2,1,0:T(2,128)(2,1)}), bf16[8,1,80]{2,1,0:T(2,128)(2,1)S(1)}, u32[]{:S(2)}, u32[]{:S(2)}) async-start(bf16[8,1,80]{2,1,0:T(2,128)(2,1)} %convert_element_type.182), calls=%async_computation.4 | async-start | bytes 8192 | tf_op jit(solution)/shard_map/all_to_all | solution.py:146
  560.7 11.7 %all-to-all-start.3 = ((bf16[8,2,7680]{2,1,0:T(2,128)(2,1)}), bf16[8,2,7680]{2,1,0:T(2,128)(2,1)S(1)}, u32[]{:S(2)}, u32[]{:S(2)}) async-start(bf16[8,2,7680]{2,1,0:T(2,128)(2,1)} %reshape.292), calls=%async_computation.3 | async-start | bytes 491520 | tf_op jit(solution)/shard_map/all_to_all | solution.py:139
  573.3 10.8 %copy-start.9 = (pred[256,2]{1,0:T(8,128)(4,1)S(1)}, pred[256,2]{1,0:T(8,128)(4,1)}, u32[]{:S(2)}) copy-start(pred[256,2]{1,0:T(8,128)(4,1)} %get-tuple-element.34) | copy-start | bytes 1540
Sparse Core Ops, SparseCore 0:
  40.9 95.2 all-gather.4
  139.3 92.2 all-gather.6
  341.0 202.8 all-reduce.3
where the time goes:
time: 603 us; the launch traced here: 594 us
  local copies, waits for them, and re-layouts  176 us (29%)
  blocking collectives  146 us (24%)
  waiting for transfers between devices  133 us (22%)
  matrix products  62 us (10%)
  starting transfers between devices  38.3 us (6%)
  other arithmetic  24 us (4%)
  between operations  14.3 us (2%)
    psum x1, blocking collectives, local(): lax.psum(back_part.astype(jnp.bfloat16), 'expert').astype(jnp.float32)  115 us
    all_gather x1, waiting for transfers between devices, local(): lax.all_gather(recv_dy[None], 'expert', axis=0, tiled=True)  65.3 us
    dot_general x15, matrix products, product(): jnp.einsum(pattern, operand_a, operand_b, preferred_element_type=jnp.floa...  53.1 us
    reshape x2, local copies, waits for them, and re-layouts, full_rows(): return ordered.reshape(n_sources * capacity, n_groups * part_width)  36.7 us
    reshape x2, local copies, waits for them, and re-layouts, full_rows(): gathered.reshape(n_groups, n_sources, capacity, part_width)  36.4 us
    all_gather x1, waiting for transfers between devices, local(): lax.all_gather(recv_x[None], 'expert', axis=0, tiled=True)  33.9 us
    all_to_all x1, starting transfers between devices, local(): lax.all_to_all(gate_dots.reshape(n_experts, capacity).astype(jnp.bfloat16...  32.7 us
    unnamed x4, waiting for transfers between devices  30.9 us
  transfers between devices with their start and end apart: 5, of which 4 were waited for; matrix products, arithmetic and copies ran while one was open for 17% of the time, Pallas kernels for 0%

commit v1 on v0

--- a/solution.py
+++ b/solution.py
@@ -4,6 +4,12 @@
 from jax.sharding import PartitionSpec as P
 
 adapter_scale = 2.0
+
+
+def add_all(block, axis):
+    pieces = lax.all_gather(block, axis, axis=0, tiled=False)
+    result = pieces.sum(axis=0)
+    return result
 
 
 def product(pattern, operand_a, operand_b):
@@ -110,7 +116,7 @@
         axis=0,
     )
     back_sum, gate_sum = (
-        lax.psum(back_part.astype(jnp.bfloat16), "expert").astype(jnp.float32),
+        add_all(back_part.astype(jnp.bfloat16), "expert").astype(jnp.float32),
         lax.psum(gate_part.astype(jnp.bfloat16), "expert").astype(jnp.float32),
     )
     low_out = out_low.astype(jnp.bfloat16)

time: 603 us -> 637 us (1.056)
  waiting for transfers between devices: 133 us -> 164 us
    unnamed x4 -> x5, waiting for transfers between devices: 30.9 us -> 64.2 us
  transfers between devices with their start and end apart: 5 -> 6, of which waited for: 4 -> 4; matrix products, arithmetic and copies ran while one was open for 17% -> 23% of each run, Pallas kernels for 0% -> 0%
where the time goes in v1:
time: 637 us; the launch traced here: 628 us
  local copies, waits for them, and re-layouts  176 us (28%)
  waiting for transfers between devices  164 us (26%)
  blocking collectives  146 us (23%)
  matrix products  62.2 us (10%)
  starting transfers between devices  38.3 us (6%)
  other arithmetic  26.9 us (4%)
  between operations  14.3 us (2%)
    psum x1, blocking collectives, local(): lax.psum(out_part.astype(jnp.bfloat16), 'expert').astype(jnp.float32)  115 us
    all_gather x1, waiting for transfers between devices, local(): lax.all_gather(recv_dy[None], 'expert', axis=0, tiled=True)  65.2 us
    unnamed x5, waiting for transfers between devices  64.2 us
    dot_general x15, matrix products, product(): jnp.einsum(pattern, operand_a, operand_b, preferred_element_type=jnp.floa...  53.4 us
    reshape x2, local copies, waits for them, and re-layouts, full_rows(): return ordered.reshape(n_sources * capacity, n_groups * part_width)  36.6 us
    reshape x2, local copies, waits for them, and re-layouts, full_rows(): gathered.reshape(n_groups, n_sources, capacity, part_width)  36.4 us
    all_gather x1, waiting for transfers between devices, local(): lax.all_gather(recv_x[None], 'expert', axis=0, tiled=True)  33.8 us
    all_to_all x1, starting transfers between devices, local(): lax.all_to_all(gate_dots.reshape(n_experts, capacity).astype(jnp.bfloat16...  33.1 us
  transfers between devices with their start and end apart: 6, of which 4 were waited for; matrix products, arithmetic and copies ran while one was open for 23% of the time, Pallas kernels for 0%

profile of v1, /device:TPU:1, one launch (start us, length us, event | category | flops | bytes accessed | tf_op | source)
XLA Modules:
  0.0 628.1 jit_solution(16361472242169310705)
XLA Ops:
  25.4 12.8 %all_to_all.38 = bf16[8,2,7680]{2,1,0:T(2,128)(2,1)S(1)} all-to-all(bf16[8,2,7680]{2,1,0:T(2,128)(2,1)} %reshape.321), channel_id=1, replica_groups=mesh['dp'=8,'expert'=32] {'dp'}, dimensions={0} | all-to-all | bytes 491520 | tf_op jit(solution)/shard_map/all_to_all | solution.py:73
  48.8 10.7 %all_to_all.39 = bf16[8,2,7680]{2,1,0:T(2,128)(2,1)S(1)} all-to-all(bf16[8,2,7680]{2,1,0:T(2,128)(2,1)} %reshape.319), channel_id=1, replica_groups=mesh['dp'=8,'expert'=32] {'dp'}, dimensions={0} | all-to-all | bytes 491520 | tf_op jit(solution)/shard_map/all_to_all | solution.py:72
  62.9 8.1 %all_to_all.40 = bf16[8,1,80]{2,1,0:T(2,128)(2,1)S(1)} all-to-all(bf16[8,1,80]{2,1,0:T(2,128)(2,1)S(1)} %convert_element_type.189), channel_id=1, replica_groups=mesh['dp'=8,'expert'=32] {'dp'}, dimensions={0} | all-to-all | bytes 2560 | tf_op jit(solution)/shard_map/all_to_all | solution.py:74
  71.1 65.2 %all-gather.8.cloned.1.call-done = bf16[256,1,15360]{2,0,1:T(8,128)(2,1)} async-done(((bf16[8,1,15360]{2,0,1:T(8,128)(2,1)}), bf16[256,1,15360]{2,0,1:T(8,128)(2,1)}) %all-gather.8.cloned.1.call-update) | async-done | bytes 7864336 | tf_op jit(solution)/shard_map/all_gather | solution.py:79
  136.3 18.1 %reshape.262 = bf16[32,8,80,192]{3,2,1,0:T(8,128)(2,1)} reshape(bf16[256,1,15360]{2,0,1:T(8,128)(2,1)} %all-gather.8.cloned.1.call-done) | data formatting | bytes 15728640 | tf_op jit(solution)/shard_map/reshape | solution.py:27
  154.4 13.9 %copy.93 = bf16[8,80,32,192]{3,2,1,0:T(8,128)(2,1)} copy(bf16[8,80,32,192]{3,1,0,2:T(8,128)(2,1)} %bitcast.107) | data formatting | bytes 15728640 | tf_op jit(solution)/shard_map/transpose | solution.py:27
  168.3 18.2 %reshape.263 = bf16[640,6144]{1,0:T(8,128)(2,1)} reshape(bf16[8,80,32,192]{3,2,1,0:T(8,128)(2,1)} %copy.93) | data formatting | bytes 15728640 | tf_op jit(solution)/shard_map/reshape | solution.py:28
  186.6 6.0 convolution_bitcast_fusion
  192.6 5.5 fusion.7
  198.0 33.8 %all-gather.10.cloned.1.call-done = bf16[256,1,15360]{2,0,1:T(8,128)(2,1)} async-done(((bf16[8,1,15360]{2,0,1:T(8,128)(2,1)}), bf16[256,1,15360]{2,0,1:T(8,128)(2,1)}) %all-gather.10.cloned.1.call-update) | async-done | bytes 7864336 | tf_op jit(solution)/shard_map/all_gather | solution.py:78
  231.8 18.3 %reshape.264 = bf16[32,8,80,192]{3,2,1,0:T(8,128)(2,1)} reshape(bf16[256,1,15360]{2,0,1:T(8,128)(2,1)} %all-gather.10.cloned.1.call-done) | data formatting | bytes 15728640 | tf_op jit(solution)/shard_map/reshape | solution.py:27
  250.1 13.8 %copy.98 = bf16[8,80,32,192]{3,2,1,0:T(8,128)(2,1)} copy(bf16[8,80,32,192]{3,1,0,2:T(8,128)(2,1)} %bitcast.108) | data formatting | bytes 15728640 | tf_op jit(solution)/shard_map/transpose | solution.py:27
  263.9 18.3 %reshape.265 = bf16[640,6144]{1,0:T(8,128)(2,1)} reshape(bf16[8,80,32,192]{3,2,1,0:T(8,128)(2,1)} %copy.98) | data formatting | bytes 15728640 | tf_op jit(solution)/shard_map/reshape | solution.py:28
  282.3 5.8 convolution_convert_fusion
  297.4 8.6 %fusion.25 = f32[640,32,192]{0,2,1:T(8,128)} fusion(bf16[32,192,256]{2,1,0:T(8,128)(2,1)S(1)} %bitcast.106, bf16[640,256]{0,1:T(8,128)(2,1)} %copy-done.7), kind=kOutput, calls=%fused_computation.53 | convolution fusion | flops 2013265920 | bytes 19202048 | tf_op jit(solution)/shard_map/nf,kdf->knd/dot_general | solution.py:16
  306.0 8.9 %fusion.2 = bf16[32,640,192]{1,2,0:T(8,128)(2,1)} fusion(f32[640,32,192]{0,2,1:T(8,128)} %fusion.25, bf16[32,192,256]{2,1,0:T(8,128)(2,1)S(1)} %bitcast.109, bf16[640,256]{0,1:T(8,128)(2,1)S(1)} %copy-done.6), kind=kOutput, calls=%fused_computation.7 | convolution fusion | flops 2021130240 | bytes 27066368 | tf_op jit(solution)/shard_map/nf,kdf->knd/dot_general | solution.py:16
  314.9 13.7 %copy.101 = bf16[32,640,192]{2,1,0:T(8,128)(2,1)} copy(bf16[32,640,192]{1,2,0:T(8,128)(2,1)} %fusion.2) | data formatting | bytes 15728640 | tf_op jit(solution)/shard_map/convert_element_type | solution.py:132
  328.6 15.5 %convert_element_type.167 = bf16[32,122880]{1,0:T(8,128)(2,1)} reshape(bf16[32,640,192]{2,1,0:T(8,128)(2,1)} %copy.101) | data formatting | bytes 15728640 | tf_op jit(solution)/shard_map/convert_element_type | solution.py:132
  347.7 114.7 %all-reduce.1 = (bf16[16,640]{1,0:T(8,128)(2,1)S(1)}, bf16[640]{0:T(1024)(128)(2,1)S(1)}) all-reduce(bf16[16,640]{1,0:T(8,128)(2,1)S(1)} %fusion.18, bf16[640]{0:T(1024)(128)(2,1)S(1)} %get-tuple-element.34), channel_id=1, replica_groups=mesh['dp'=8,'expert'=32] {'expert'}, use_global_device_ids=true, to_apply=%region_9.10 | all-reduce | flops 10880 | bytes 43520 | tf_op jit(solution)/shard_map/psum | solution.py:101
  463.1 33.1 %all-to-all-start.4 = ((bf16[8,1,80]{2,1,0:T(2,128)(2,1)}), bf16[8,1,80]{2,1,0:T(2,128)(2,1)S(1)}, u32[]{:S(2)}, u32[]{:S(2)}) async-start(bf16[8,1,80]{2,1,0:T(2,128)(2,1)} %convert_element_type.191), calls=%async_computation.4 | async-start | bytes 8192 | tf_op jit(solution)/shard_map/all_to_all | solution.py:152
  500.4 5.1 fusion.1
  514.0 64.1 %all-reduce.4.cloned.1.call-done = bf16[32,122880]{1,0:T(8,128)(2,1)} async-done(((bf16[32,122880]{1,0:T(8,128)(2,1)}), bf16[32,122880]{1,0:T(8,128)(2,1)}) %all-reduce.4.cloned.1.call-update) | async-done | bytes 7864336
  595.1 5.1 all-to-all-start.3
  600.2 5.6 fusion
  (118 shorter events, 91.0 us)
Async XLA Ops:
  7.2 280.9 %copy-start = (bf16[1,6144,256]{2,1,0:T(8,128)(2,1)S(1)}, bf16[1,6144,256]{2,1,0:T(8,128)(2,1)}, u32[]{:S(2)}) copy-start(bf16[1,6144,256]{2,1,0:T(8,128)(2,1)} %param.15) | copy-start | bytes 9437188
  7.2 55.1 %copy-start.12 = (bf16[256,2]{0,1:T(2,128)(2,1)S(1)}, bf16[256,2]{0,1:T(2,128)(2,1)}, u32[]{:S(2)}) copy-start(bf16[256,2]{0,1:T(2,128)(2,1)} %param.14) | copy-start | bytes 3076
  7.2 129.1 %all-gather.8.cloned.1.call-start = ((), (), s32[]{:S(2)}) async-start(), calls=%async_computation.6 | async-start | bytes 8110080 | tf_op jit(solution)/shard_map/all_gather | solution.py:79
  40.9 190.9 %all-gather.10.cloned.1.call-start = ((), (), s32[]{:S(2)}) async-start(), calls=%async_computation.7 | async-start | bytes 8110080 | tf_op jit(solution)/shard_map/all_gather | solution.py:78
  62.3 450.3 %all-gather.6.cloned.1.call-start = ((), (), s32[]{:S(2)}) async-start(), calls=%async_computation.5 | async-start | bytes 1351680 | tf_op jit(solution)/shard_map/all_gather | solution.py:10
  168.3 18.2 %copy-start.9 = (bf16[1,16,6144]{2,1,0:T(8,128)(2,1)S(1)}, bf16[1,16,6144]{2,1,0:T(8,128)(2,1)}, u32[]{:S(2)}) copy-start(bf16[1,16,6144]{2,1,0:T(8,128)(2,1)} %param.21) | copy-start | bytes 589828
  186.6 6.0 copy-start.2
  282.3 5.8 copy-start.1
  288.1 2.9 copy-start.3
  291.0 2.9 copy-start.10
  291.0 3.2 copy-start.8
  291.0 3.2 copy-start.11
  295.8 0.7 copy-start.5
  295.8 0.9 copy-start.7
  297.4 280.8 %all-reduce.4.cloned.1.call-start = ((), (), s32[]{:S(2)}) async-start(), calls=%async_computation.8 | async-start | bytes 15728640
  297.4 8.6 %copy-start.4 = (bf16[1,6144,256]{2,1,0:T(8,128)(2,1)S(1)}, bf16[1,6144,256]{2,1,0:T(8,128)(2,1)}, u32[]{:S(2)}) copy-start(bf16[1,6144,256]{2,1,0:T(8,128)(2,1)} %param.16) | copy-start | bytes 9437188
  297.4 8.6 %copy-start.6 = (bf16[640,256]{0,1:T(8,128)(2,1)S(1)}, bf16[640,256]{0,1:T(8,128)(2,1)}, u32[]{:S(2)}) copy-start(bf16[640,256]{0,1:T(8,128)(2,1)} %copy-done.5) | copy-start | bytes 983044
  344.0 1.9 copy-start.13
  463.1 43.0 %all-to-all-start.4 = ((bf16[8,1,80]{2,1,0:T(2,128)(2,1)}), bf16[8,1,80]{2,1,0:T(2,128)(2,1)S(1)}, u32[]{:S(2)}, u32[]{:S(2)}) async-start(bf16[8,1,80]{2,1,0:T(2,128)(2,1)} %convert_element_type.191), calls=%async_computation.4 | async-start | bytes 8192 | tf_op jit(solution)/shard_map/all_to_all | solution.py:152
  595.1 11.4 %all-to-all-start.3 = ((bf16[8,2,7680]{2,1,0:T(2,128)(2,1)}), bf16[8,2,7680]{2,1,0:T(2,128)(2,1)S(1)}, u32[]{:S(2)}, u32[]{:S(2)}) async-start(bf16[8,2,7680]{2,1,0:T(2,128)(2,1)} %reshape.323), calls=%async_computation.3 | async-start | bytes 491520 | tf_op jit(solution)/shard_map/all_to_all | solution.py:145
Sparse Core Ops, SparseCore 0:
  41.0 95.2 all-gather.7
  139.5 92.2 all-gather.9
  297.5 69.9 all-gather.5
  371.0 207.1 all-reduce.3
